TPU v7x, 512 devices: a whole 4x8x8 slice. The times are simulated.
512 devices in a mesh: panel: 32 (over y_lo, z, core), rhs: 16 (over x, y_hi).
Axes of the slice: x: 4, y: 8 (y_hi: 4, y_lo: 2; y = y_hi * 2 + y_lo), z: 8, core: 2. Of those that a mesh axis runs over, the one named last changes fastest.
Arguments:
- pivot_rhs: float32 [2, 2048, 2048], P(None, 'panel', 'rhs'), may hold values from -6 to 6
- update_rhs: float32 [4096, 2048], P('panel', 'rhs'), may hold values from -6 to 6
- parent_rhs: float32 [4096, 2048], P('panel', 'rhs'), may hold values from -6 to 6
- lower_pivot: bfloat16 [2, 2048, 2048], P(None, 'panel', 'rhs'), may hold values from -1 to 1.4, as said below
- lower_update: bfloat16 [4096, 2048], P('panel', 'rhs'), may hold values from -0.125 to 0.125
- parent_lower: bfloat16 [4096, 4096], P('panel', 'rhs'), may hold values from -1 to 1.4, as said below
- parent_upper: bfloat16 [4096, 4096], P('panel', 'rhs'), may hold values from -1 to 1.4, as said below
- upper_pivot: bfloat16 [2, 2048, 2048], P(None, 'panel', 'rhs'), may hold values from -1 to 1.4, as said below
- upper_update: bfloat16 [2, 2048, 2048], P(None, 'panel', 'rhs'), may hold values from -0.125 to 0.125
- maps: int32 [4096], replicated, may hold values from 0 to 4095, as said below
Outputs:
- parent_solution: float32 [4096, 2048], P('panel', 'rhs')
- child_solution: float32 [2, 2048, 2048], P(None, 'panel', 'rhs')
Inputs may be any that keep to these rules, and one draw needn't show every extreme that they name: `maps`: for each child k, entry k * 2048 + i is 2 * i + b with b equal to 0 or 1; both values of b occur for each child in every draw. `lower_pivot`: each block is lower triangular, diagonal 0.6 to 1.4. `upper_pivot`: each block is upper triangular, diagonal 0.6 to 1.4. `parent_lower`: lower triangular, diagonal 0.6 to 1.4. `parent_upper`: upper triangular, diagonal 0.6 to 1.4.
All inputs are finite; a program needn't handle non-finite values.
Results may differ from a plain program's by a relative error of at most 0.0054.
Values may be sent and summed in bfloat16 or wider, within the bound.
A program may use at most 64 MiB of HBM per device.

v0:
```python
import jax
import jax.numpy as jnp
from jax import lax
from jax.sharding import PartitionSpec as P

FU = 2048


def copy_for_each(shard, axis):
    peers = lax.axis_size(axis)
    return lax.all_to_all(
        jnp.broadcast_to(shard[None], (peers, *shard.shape)), axis, 0, 0, tiled=True
    )


def laid_out(blocks, dim):
    blocks = jnp.moveaxis(blocks, 0, dim)
    lengths = blocks.shape
    return blocks.reshape(*lengths[:dim], lengths[dim] * lengths[dim + 1], *lengths[dim + 2 :])


def collect(shard, axis, dim):
    blocks = copy_for_each(shard, axis)
    return laid_out(blocks, dim)


def sent_together(arrays, axis, dim, along):
    ends, at = ([], 0)
    for a in arrays[:-1]:
        at += a.shape[along]
        ends.append(at)
    both = jnp.concatenate(arrays, axis=along)
    return tuple(jnp.split(lax.all_gather(both, axis, axis=dim, tiled=True), ends, axis=along))


def product(left, right):
    return jnp.dot(left, right, preferred_element_type=jnp.float32)


def paired(left, right):
    return jnp.einsum("kqw,kwr->kqr", left, right, preferred_element_type=jnp.float32)


def through(factor, vector):
    return product(collect(factor, "rhs", 1), vector)


def shards(
    pivot_rhs,
    update_rhs,
    parent_rhs,
    lower_pivot,
    lower_update,
    parent_lower,
    parent_upper,
    upper_pivot,
    upper_update,
    maps,
):
    panel_index = lax.axis_index("panel")
    row_count = update_rhs.shape[0]
    rhs_width = update_rhs.shape[1]
    pivot_local = pivot_rhs.shape[1]
    first_row = panel_index * row_count
    child_index = first_row // FU
    pivot_all = collect(pivot_rhs.astype(jnp.bfloat16), "panel", 1)
    own_rhs = lax.dynamic_index_in_dim(pivot_all, child_index, 0, keepdims=False)
    lower_flat = lower_pivot.reshape(2 * pivot_local, lower_pivot.shape[2])
    pieces = sent_together((lower_flat, lower_update), "rhs", 1, 0)
    width = pieces[0].shape[1]
    blocks = pieces[0].reshape(2, pivot_local, width)
    pivot_mid = paired(blocks, pivot_all)
    update_sum = product(pieces[1], own_rhs)
    update_half = (update_rhs + update_sum).astype(jnp.bfloat16)
    pivot_half = pivot_mid.astype(jnp.bfloat16)
    pivot_known = collect(pivot_half, "panel", 1)
    own_rows = first_row + lax.broadcasted_iota(jnp.int32, (row_count, 1), 0)
    select = (own_rows == maps[None, :]).astype(jnp.bfloat16)
    parent_sum = parent_rhs + product(select, collect(update_half, "panel", 0))
    parent_all = collect(parent_sum.astype(jnp.bfloat16), "panel", 0)
    parent_mid = through(parent_lower, parent_all)
    middle_all = collect(parent_mid.astype(jnp.bfloat16), "panel", 0)
    parent_solution = through(parent_upper, middle_all)
    solution_half = parent_solution.astype(jnp.bfloat16)
    solution_all = collect(solution_half, "panel", 0)
    remote_rows = jnp.take(solution_all, maps, axis=0).reshape(2, FU, rhs_width)
    pieces = sent_together((upper_pivot, upper_update), "rhs", 2, 0)
    child_solution = paired(pieces[0], pivot_known) + paired(pieces[1], remote_rows)
    return (parent_solution, child_solution)


def solution(mesh):
    placed = (
        P(None, "panel", "rhs"),
        P("panel", "rhs"),
        P("panel", "rhs"),
        P(None, "panel", "rhs"),
        P("panel", "rhs"),
        P("panel", "rhs"),
        P("panel", "rhs"),
        P(None, "panel", "rhs"),
        P(None, "panel", "rhs"),
        P(),
    )
    return jax.shard_map(
        shards,
        mesh=mesh,
        in_specs=placed,
        out_specs=(P("panel", "rhs"), P(None, "panel", "rhs")),
        check_vma=False,
    )
```

profile of v0, /device:TPU:1, one launch (start us, length us, event | category | flops | bytes accessed | tf_op | source)
XLA Modules:
  0.0 352.0 jit_solution(16716216847756293906)
XLA Ops:
  7.2 0.8 convert_element_type.22
  8.0 1.2 broadcast_in_dim.27
  9.2 0.0 copy-start.6
  9.2 0.0 copy-start.7
  9.2 13.1 %all-to-all-start = ((bf16[32,2,64,128]{3,2,1,0:T(8,128)(2,1)}), bf16[32,2,64,128]{3,2,1,0:T(8,128)(2,1)S(1)}, u32[]{:S(2)}, u32[]{:S(2)}) async-start(bf16[32,2,64,128]{3,2,1,0:T(8,128)(2,1)} %broadcast_in_dim.27), calls=%async_computation | async-start | bytes 2097152 | tf_op jit(solution)/shard_map/all_to_all | solution.py:11
  22.3 0.0 all-gather.3.cloned.1.call-start
  22.4 0.0 copy-done.6
  22.4 0.0 copy-done.7
  22.4 0.6 pad_maximum_fusion
  23.1 0.0 all-gather.3.cloned.1.call-update
  23.1 26.2 %all-to-all-done = bf16[32,2,64,128]{3,2,1,0:T(8,128)(2,1)S(1)} async-done(((bf16[32,2,64,128]{3,2,1,0:T(8,128)(2,1)}), bf16[32,2,64,128]{3,2,1,0:T(8,128)(2,1)S(1)}, u32[]{:S(2)}, u32[]{:S(2)}) %all-to-all-start) | async-done | bytes 1048608 | tf_op jit(solution)/shard_map/all_to_all | solution.py:11
  49.3 0.0 copy-start.2
  49.3 0.1 copy.20
  49.4 34.8 %all-gather.3.cloned.1.call-done = bf16[256,2048]{1,0:T(8,128)(2,1)} async-done(((bf16[256,128]{1,0:T(8,128)(2,1)}), bf16[256,2048]{1,0:T(8,128)(2,1)}) %all-gather.3.cloned.1.call-update) | async-done | bytes 1048592 | tf_op jit(solution)/shard_map/all_gather | solution.py:33
  84.2 0.0 copy-done.2
  84.2 1.3 fusion.5
  85.5 1.2 broadcast_in_dim.28
  86.7 10.5 %all-to-all-start.1 = ((bf16[32,128,128]{2,1,0:T(8,128)(2,1)}), bf16[32,128,128]{2,1,0:T(8,128)(2,1)S(1)}, u32[]{:S(2)}, u32[]{:S(2)}) async-start(bf16[32,128,128]{2,1,0:T(8,128)(2,1)} %broadcast_in_dim.28), calls=%async_computation.1 | async-start | bytes 2097152 | tf_op jit(solution)/shard_map/all_to_all | solution.py:11
  97.2 0.0 copy-done.4
  97.2 0.1 copy.21
  97.3 26.8 %all-to-all-done.1 = bf16[32,128,128]{2,1,0:T(8,128)(2,1)S(1)} async-done(((bf16[32,128,128]{2,1,0:T(8,128)(2,1)}), bf16[32,128,128]{2,1,0:T(8,128)(2,1)S(1)}, u32[]{:S(2)}, u32[]{:S(2)}) %all-to-all-start.1) | async-done | bytes 1048608 | tf_op jit(solution)/shard_map/all_to_all | solution.py:11
  124.1 1.2 broadcast_in_dim.30
  125.3 6.0 %all-to-all-start.3 = ((bf16[16,128,256]{1,2,0:T(8,128)(2,1)}), bf16[16,128,256]{1,2,0:T(8,128)(2,1)S(1)}, u32[]{:S(2)}, u32[]{:S(2)}) async-start(bf16[16,128,256]{1,2,0:T(8,128)(2,1)} %broadcast_in_dim.30), calls=%async_computation.3 | async-start | bytes 2097152 | tf_op jit(solution)/shard_map/all_to_all | solution.py:11
  131.3 0.0 copy-done.3
  131.3 0.0 copy-done.10
  131.4 0.5 fusion.6
  131.9 24.4 %all-to-all-done.3 = bf16[16,128,256]{1,2,0:T(8,128)(2,1)S(1)} async-done(((bf16[16,128,256]{1,2,0:T(8,128)(2,1)}), bf16[16,128,256]{1,2,0:T(8,128)(2,1)S(1)}, u32[]{:S(2)}, u32[]{:S(2)}) %all-to-all-start.3) | async-done | bytes 1048608 | tf_op jit(solution)/shard_map/all_to_all | solution.py:11
  156.3 1.2 broadcast_in_dim.29
  157.5 10.8 %all-to-all-start.2 = ((bf16[32,128,128]{2,1,0:T(8,128)(2,1)}), bf16[32,128,128]{2,1,0:T(8,128)(2,1)S(1)}, u32[]{:S(2)}, u32[]{:S(2)}) async-start(bf16[32,128,128]{2,1,0:T(8,128)(2,1)} %broadcast_in_dim.29), calls=%async_computation.2 | async-start | bytes 2097152 | tf_op jit(solution)/shard_map/all_to_all | solution.py:11
  168.4 0.0 copy-done.5
  168.4 0.1 copy.23
  168.5 26.8 %all-to-all-done.2 = bf16[32,128,128]{2,1,0:T(8,128)(2,1)S(1)} async-done(((bf16[32,128,128]{2,1,0:T(8,128)(2,1)}), bf16[32,128,128]{2,1,0:T(8,128)(2,1)S(1)}, u32[]{:S(2)}, u32[]{:S(2)}) %all-to-all-start.2) | async-done | bytes 1048608 | tf_op jit(solution)/shard_map/all_to_all | solution.py:11
  195.3 1.3 broadcast_in_dim.32
  196.6 0.0 copy-done
  196.6 3.7 %all-to-all-start.5 = ((bf16[16,128,256]{1,2,0:T(8,128)(2,1)}), bf16[16,128,256]{1,2,0:T(8,128)(2,1)S(1)}, u32[]{:S(2)}, u32[]{:S(2)}) async-start(bf16[16,128,256]{1,2,0:T(8,128)(2,1)} %broadcast_in_dim.32), calls=%async_computation.5 | async-start | bytes 2097152 | tf_op jit(solution)/shard_map/all_to_all | solution.py:11
  200.3 1.7 fusion.9
  202.0 0.1 copy.22
  202.1 23.1 %all-to-all-done.5 = bf16[16,128,256]{1,2,0:T(8,128)(2,1)S(1)} async-done(((bf16[16,128,256]{1,2,0:T(8,128)(2,1)}), bf16[16,128,256]{1,2,0:T(8,128)(2,1)S(1)}, u32[]{:S(2)}, u32[]{:S(2)}) %all-to-all-start.5) | async-done | bytes 1048608 | tf_op jit(solution)/shard_map/all_to_all | solution.py:11
  225.2 1.2 broadcast_in_dim.31
  226.4 10.9 %all-to-all-start.4 = ((bf16[32,128,128]{2,1,0:T(8,128)(2,1)}), bf16[32,128,128]{2,1,0:T(8,128)(2,1)S(1)}, u32[]{:S(2)}, u32[]{:S(2)}) async-start(bf16[32,128,128]{2,1,0:T(8,128)(2,1)} %broadcast_in_dim.31), calls=%async_computation.4 | async-start | bytes 2097152 | tf_op jit(solution)/shard_map/all_to_all | solution.py:11
  237.3 0.0 slice-start
  237.3 1.0 slice-done
  238.3 0.3 convolution_convert_fusion
  238.7 25.5 %all-to-all-done.4 = bf16[32,128,128]{2,1,0:T(8,128)(2,1)S(1)} async-done(((bf16[32,128,128]{2,1,0:T(8,128)(2,1)}), bf16[32,128,128]{2,1,0:T(8,128)(2,1)S(1)}, u32[]{:S(2)}, u32[]{:S(2)}) %all-to-all-start.4) | async-done | bytes 1048608 | tf_op jit(solution)/shard_map/all_to_all | solution.py:11
  264.2 1.2 broadcast_in_dim.33
  265.4 5.6 %all-to-all-start.6 = ((bf16[32,2,64,128]{3,2,1,0:T(8,128)(2,1)}), bf16[32,2,64,128]{3,2,1,0:T(8,128)(2,1)S(1)}, u32[]{:S(2)}, u32[]{:S(2)}) async-start(bf16[32,2,64,128]{3,2,1,0:T(8,128)(2,1)} %broadcast_in_dim.33), calls=%async_computation.6 | async-start | bytes 2097152 | tf_op jit(solution)/shard_map/all_to_all | solution.py:11
  271.0 0.0 all-gather.5.cloned.1.call-start
  271.1 0.0 copy-done.8
  271.1 0.0 copy-done.9
  271.1 0.6 pad_maximum_fusion.1
  271.7 0.0 all-gather.5.cloned.1.call-update
  271.8 0.5 fusion.21
  272.2 0.1 copy.25
  272.4 25.6 %all-to-all-done.6 = bf16[32,2,64,128]{3,2,1,0:T(8,128)(2,1)S(1)} async-done(((bf16[32,2,64,128]{3,2,1,0:T(8,128)(2,1)}), bf16[32,2,64,128]{3,2,1,0:T(8,128)(2,1)S(1)}, u32[]{:S(2)}, u32[]{:S(2)}) %all-to-all-start.6) | async-done | bytes 1048608 | tf_op jit(solution)/shard_map/all_to_all | solution.py:11
  297.9 1.2 broadcast_in_dim.72
  299.1 5.4 %all-to-all-start.7 = ((bf16[32,128,128]{2,1,0:T(8,128)(2,1)}), bf16[32,128,128]{2,1,0:T(8,128)(2,1)S(1)}, u32[]{:S(2)}, u32[]{:S(2)}) async-start(bf16[32,128,128]{2,1,0:T(8,128)(2,1)} %broadcast_in_dim.72), calls=%async_computation.7 | async-start | bytes 2097152 | tf_op jit(solution)/shard_map/all_to_all | solution.py:11
  304.6 0.1 copy.24
  304.7 24.2 %all-gather.5.cloned.1.call-done = bf16[4,64,2048]{2,1,0:T(8,128)(2,1)} async-done(((bf16[4,64,128]{2,1,0:T(8,128)(2,1)}), bf16[4,64,2048]{2,1,0:T(8,128)(2,1)}) %all-gather.5.cloned.1.call-update) | async-done | bytes 1048592 | tf_op jit(solution)/shard_map/all_gather | solution.py:33
  329.0 1.3 fusion.22
  330.3 0.7 copy.26
  331.0 0.6 all-to-all-done.7
  331.7 12.1 %gather_fusion = bf16[4096,128]{1,0:T(8,128)(2,1)S(1)} fusion(bf16[4096,128]{1,0:T(8,128)(2,1)S(1)} %bitcast.34, s32[4096]{0:T(1024)S(1)} %fusion.18), kind=kCustom, calls=%fused_computation | custom fusion | bytes 2113536 | tf_op jit(solution)/shard_map/jit(_take)/gather | solution.py:86
  343.8 0.0 copy-done.1
  343.8 1.4 convolution_add_fusion
  (12 shorter events, 0.0 us)
Async XLA Ops:
  9.2 13.2 %copy-start.6 = (bf16[128,128]{1,0:T(8,128)(2,1)S(1)}, bf16[128,128]{1,0:T(8,128)(2,1)}, u32[]{:S(2)}) copy-start(bf16[128,128]{1,0:T(8,128)(2,1)} %param.14) | copy-start | bytes 98308
  9.2 13.2 %copy-start.7 = (bf16[2,64,128]{2,1,0:T(8,128)(2,1)S(1)}, bf16[2,64,128]{2,1,0:T(8,128)(2,1)}, u32[]{:S(2)}) copy-start(bf16[2,64,128]{2,1,0:T(8,128)(2,1)} %param.13) | copy-start | bytes 98308
  9.2 40.0 %all-to-all-start = ((bf16[32,2,64,128]{3,2,1,0:T(8,128)(2,1)}), bf16[32,2,64,128]{3,2,1,0:T(8,128)(2,1)S(1)}, u32[]{:S(2)}, u32[]{:S(2)}) async-start(bf16[32,2,64,128]{3,2,1,0:T(8,128)(2,1)} %broadcast_in_dim.27), calls=%async_computation | async-start | bytes 2097152 | tf_op jit(solution)/shard_map/all_to_all | solution.py:11
  22.3 61.8 %all-gather.3.cloned.1.call-start = ((), (), s32[]{:S(2)}) async-start(), calls=%async_computation.8 | async-start | bytes 1114112 | tf_op jit(solution)/shard_map/all_gather | solution.py:33
  49.3 34.9 %copy-start.2 = (f32[128,128]{1,0:T(8,128)S(1)}, f32[128,128]{1,0:T(8,128)}, u32[]{:S(2)}) copy-start(f32[128,128]{1,0:T(8,128)} %param.11) | copy-start | bytes 196612
  86.7 10.5 %copy-start.4 = (bf16[128,256]{1,0:T(8,128)(2,1)S(1)}, bf16[128,256]{1,0:T(8,128)(2,1)}, u32[]{:S(2)}) copy-start(bf16[128,256]{1,0:T(8,128)(2,1)} %param.15) | copy-start | bytes 196612
  86.7 37.4 %all-to-all-start.1 = ((bf16[32,128,128]{2,1,0:T(8,128)(2,1)}), bf16[32,128,128]{2,1,0:T(8,128)(2,1)S(1)}, u32[]{:S(2)}, u32[]{:S(2)}) async-start(bf16[32,128,128]{2,1,0:T(8,128)(2,1)} %broadcast_in_dim.28), calls=%async_computation.1 | async-start | bytes 2097152 | tf_op jit(solution)/shard_map/all_to_all | solution.py:11
  125.3 6.1 %copy-start.3 = (s32[4096]{0:T(1024)S(1)}, s32[4096]{0:T(1024)}, u32[]{:S(2)}) copy-start(s32[4096]{0:T(1024)} %param.19) | copy-start | bytes 49156
  125.3 6.1 %copy-start.10 = (f32[128,128]{1,0:T(8,128)S(1)}, f32[128,128]{1,0:T(8,128)}, u32[]{:S(2)}) copy-start(f32[128,128]{1,0:T(8,128)} %param.12) | copy-start | bytes 196612
  125.3 31.1 %all-to-all-start.3 = ((bf16[16,128,256]{1,2,0:T(8,128)(2,1)}), bf16[16,128,256]{1,2,0:T(8,128)(2,1)S(1)}, u32[]{:S(2)}, u32[]{:S(2)}) async-start(bf16[16,128,256]{1,2,0:T(8,128)(2,1)} %broadcast_in_dim.30), calls=%async_computation.3 | async-start | bytes 2097152 | tf_op jit(solution)/shard_map/all_to_all | solution.py:11
  157.5 10.9 %copy-start.5 = (bf16[128,256]{1,0:T(8,128)(2,1)S(1)}, bf16[128,256]{1,0:T(8,128)(2,1)}, u32[]{:S(2)}) copy-start(bf16[128,256]{1,0:T(8,128)(2,1)} %param.16) | copy-start | bytes 196612
  157.5 37.8 %all-to-all-start.2 = ((bf16[32,128,128]{2,1,0:T(8,128)(2,1)}), bf16[32,128,128]{2,1,0:T(8,128)(2,1)S(1)}, u32[]{:S(2)}, u32[]{:S(2)}) async-start(bf16[32,128,128]{2,1,0:T(8,128)(2,1)} %broadcast_in_dim.29), calls=%async_computation.2 | async-start | bytes 2097152 | tf_op jit(solution)/shard_map/all_to_all | solution.py:11
  195.3 1.3 copy-start
  196.6 28.6 %all-to-all-start.5 = ((bf16[16,128,256]{1,2,0:T(8,128)(2,1)}), bf16[16,128,256]{1,2,0:T(8,128)(2,1)S(1)}, u32[]{:S(2)}, u32[]{:S(2)}) async-start(bf16[16,128,256]{1,2,0:T(8,128)(2,1)} %broadcast_in_dim.32), calls=%async_computation.5 | async-start | bytes 2097152 | tf_op jit(solution)/shard_map/all_to_all | solution.py:11
  226.4 37.8 %all-to-all-start.4 = ((bf16[32,128,128]{2,1,0:T(8,128)(2,1)}), bf16[32,128,128]{2,1,0:T(8,128)(2,1)S(1)}, u32[]{:S(2)}, u32[]{:S(2)}) async-start(bf16[32,128,128]{2,1,0:T(8,128)(2,1)} %broadcast_in_dim.31), calls=%async_computation.4 | async-start | bytes 2097152 | tf_op jit(solution)/shard_map/all_to_all | solution.py:11
  237.3 1.0 slice-start
  265.4 5.6 %copy-start.8 = (bf16[2,64,128]{2,1,0:T(8,128)(2,1)S(1)}, bf16[2,64,128]{2,1,0:T(8,128)(2,1)}, u32[]{:S(2)}) copy-start(bf16[2,64,128]{2,1,0:T(8,128)(2,1)} %param.18) | copy-start | bytes 98308
  265.4 5.6 %copy-start.9 = (bf16[2,64,128]{2,1,0:T(8,128)(2,1)S(1)}, bf16[2,64,128]{2,1,0:T(8,128)(2,1)}, u32[]{:S(2)}) copy-start(bf16[2,64,128]{2,1,0:T(8,128)(2,1)} %param.17) | copy-start | bytes 98308
  265.4 32.5 %all-to-all-start.6 = ((bf16[32,2,64,128]{3,2,1,0:T(8,128)(2,1)}), bf16[32,2,64,128]{3,2,1,0:T(8,128)(2,1)S(1)}, u32[]{:S(2)}, u32[]{:S(2)}) async-start(bf16[32,2,64,128]{3,2,1,0:T(8,128)(2,1)} %broadcast_in_dim.33), calls=%async_computation.6 | async-start | bytes 2097152 | tf_op jit(solution)/shard_map/all_to_all | solution.py:11
  271.0 57.9 %all-gather.5.cloned.1.call-start = ((), (), s32[]{:S(2)}) async-start(), calls=%async_computation.9 | async-start | bytes 1114112 | tf_op jit(solution)/shard_map/all_gather | solution.py:33
  299.1 32.5 %all-to-all-start.7 = ((bf16[32,128,128]{2,1,0:T(8,128)(2,1)}), bf16[32,128,128]{2,1,0:T(8,128)(2,1)S(1)}, u32[]{:S(2)}, u32[]{:S(2)}) async-start(bf16[32,128,128]{2,1,0:T(8,128)(2,1)} %broadcast_in_dim.72), calls=%async_computation.7 | async-start | bytes 2097152 | tf_op jit(solution)/shard_map/all_to_all | solution.py:11
  331.7 12.1 %copy-start.1 = (bf16[4,64,2048]{2,1,0:T(8,128)(2,1)S(1)}, bf16[4,64,2048]{2,1,0:T(8,128)(2,1)}, u32[]{:S(2)}) copy-start(bf16[4,64,2048]{2,1,0:T(8,128)(2,1)} %all-gather.5.cloned.1.call-done) | copy-start | bytes 3145732
Sparse Core Ops, SparseCore 0:
  26.7 57.4 all-gather.2
  275.4 53.5 all-gather.4
where the time goes:
time: 353 us; the launch traced here: 352 us
  waiting for transfers between devices  238 us (67%)
  starting transfers between devices  66.1 us (19%)
  local copies, waits for them, and re-layouts  24.2 us (7%)
  between operations  14.3 us (4%)
  matrix products  7.12 us (2%)
    all_to_all x8, waiting for transfers between devices, copy_for_each(): lax.all_to_all(jnp.broadcast_to(shard[None], (peers, *shard.shape)), axis...  179 us
    all_to_all x8, starting transfers between devices, copy_for_each(): lax.all_to_all(jnp.broadcast_to(shard[None], (peers, *shard.shape)), axis...  66 us
    all_gather x2, waiting for transfers between devices, sent_together(): lax.all_gather(both, axis, axis=dim, tiled=True)  59 us
    gather x1, local copies, waits for them, and re-layouts, shards(): remote_rows = jnp.take(solution_all, maps, axis=0).reshape(2, FU, rhs_width)  12.1 us
    broadcast_in_dim x8, local copies, waits for them, and re-layouts, copy_for_each(): jnp.broadcast_to(shard[None], (peers, *shard.shape))  9.72 us
  transfers between devices with their start and end apart: 10, of which 10 were waited for; matrix products, arithmetic and copies ran while one was open for 2% of the time, Pallas kernels for 0%

commit v1 on v0

v1 whole, which is shorter than its diff:
```python
import jax
import jax.numpy as jnp
from jax import lax
from jax.experimental import pallas as pl
from jax.experimental.pallas import tpu as pltpu
from jax.sharding import PartitionSpec as P

MESH = pl.DeviceIdType.MESH
BF = jnp.bfloat16
F32 = jnp.float32
NZ = 8
NP = 32
NQ = 16
NT = (((1,), (1,)), ((), ()))
NN = (((1,), (0,)), ((), ()))

LU, LP, PLO, PUP, UP, UU = range(6)


def dot(a, b, dims):
    return lax.dot_general(a, b, dims, preferred_element_type=F32)


def body(
    pivot_ref, update_ref, parent_ref, lp_ref, lu_ref, pl_ref, pu_ref, up_ref, uu_ref, maps_ref,
    sol_ref, child_ref,
    v, fs, fl, lu_in, upd_in, lu_out,
    g_send, g_recv, f_send, f_recv, m_send, m_recv,
):
    p = lax.axis_index("panel")
    q = lax.axis_index("rhs")
    yl = p // 16
    z = lax.rem(p // 2, NZ)
    c = lax.rem(p, 2)
    t = p // 2
    x = q // 4
    yh = lax.rem(q, 4)

    def panel_of(yl_, z_, c_):
        return yl_ * 16 + z_ * 2 + c_

    def z_at(d):
        return lax.rem(z + d, NZ)

    def q_at(dx, dy):
        return lax.rem(x + dx, 4) * 4 + lax.rem(yh + dy, 4)

    def signal(dev, sem):
        pl.semaphore_signal(sem, inc=1, device_id=dev, device_id_type=MESH)

    def fblock(a, qq):
        if a == PLO:
            return fl.at[0, pl.ds(2 * qq, 2)]
        if a == PUP:
            return fl.at[1, pl.ds(2 * qq, 2)]
        return fs.at[{LU: 0, LP: 1, UP: 2, UU: 3}[a], pl.ds(2 * qq, 2)]

    def needed(a, qq):
        if a in (LP, PLO):
            return qq <= t
        if a in (PUP, UP):
            return qq >= t
        return None

    def when(cond, fn):
        if cond is None:
            fn()
        else:
            pl.when(cond)(fn)

    def fcopy(a, qq, dev, sidx):
        return pltpu.make_async_remote_copy(
            src_ref=fblock(a, qq), dst_ref=fblock(a, qq),
            send_sem=f_send.at[a, sidx], recv_sem=f_recv.at[a, qq],
            device_id=dev, device_id_type=MESH,
        )

    def y_phase(a):
        def go():
            for i, dy in enumerate((1, 3, 2)):
                fcopy(a, q, (p, q_at(0, dy)), i).start()
            for i, dx in enumerate((1, 3, 2)):
                fcopy(a, q, (p, q_at(dx, 0)), 3 + i).start()
        when(needed(a, q), go)

    def x_phase(a):
        for j, dy in enumerate((1, 3, 2)):
            qq = q_at(0, dy)

            def go(j=j, dy=dy, qq=qq):
                fcopy(a, qq, (p, q), 0).wait_recv()
                for i, dx in enumerate((1, 3, 2)):
                    fcopy(a, qq, (p, q_at(dx, 0)), 6 + 3 * j + i).start()
            when(needed(a, qq), go)

    def f_wait(a):
        for dx in (1, 3, 2):
            for dy in range(4):
                qq = q_at(dx, dy)
                when(needed(a, qq), lambda qq=qq: fcopy(a, qq, (p, q), 0).wait_recv())

    def f_drain(a):
        def own():
            for i in range(6):
                fcopy(a, q, (p, q), i).wait_send()
        when(needed(a, q), own)
        for j, dy in enumerate((1, 3, 2)):
            qq = q_at(0, dy)

            def go(j=j, qq=qq):
                for i in range(3):
                    fcopy(a, qq, (p, q), 6 + 3 * j + i).wait_send()
            when(needed(a, qq), go)

    def gcopy(s, b, dev):
        return pltpu.make_async_remote_copy(
            src_ref=v.at[s, b], dst_ref=v.at[s, b],
            send_sem=g_send.at[s], recv_sem=g_recv.at[s, b],
            device_id=dev, device_id_type=MESH,
        )

    ydev = (panel_of(1 - yl, z, c), q)
    cdev = (panel_of(yl, z, 1 - c), q)
    ZORDER = (1, 7, 2, 6, 3, 5, 4)

    def g_start(s):
        for d in ZORDER:
            gcopy(s, p, (panel_of(yl, z_at(d), c), q)).start()
        gcopy(s, p, ydev).start()
        gcopy(s, p, cdev).start()

    def g_mid(s):
        for d in ZORDER:
            b = panel_of(yl, z_at(d), c)
            gcopy(s, b, cdev).wait_recv()
            gcopy(s, b, ydev).start()
            gcopy(s, b, cdev).start()

    def g_end(s):
        for d in (0,) + ZORDER:
            b = panel_of(1 - yl, z_at(d), c)
            gcopy(s, b, cdev).wait_recv()
            gcopy(s, b, cdev).start()
        for d in (0,) + ZORDER:
            gcopy(s, panel_of(yl, z_at(d), 1 - c), cdev).wait_recv()
        for d in (0,) + ZORDER:
            gcopy(s, panel_of(1 - yl, z_at(d), 1 - c), cdev).wait_recv()

    def g_drain(s):
        pltpu.make_async_remote_copy(
            src_ref=v.at[s, pl.ds(0, 31)], dst_ref=v.at[s, pl.ds(0, 31)],
            send_sem=g_send.at[s], recv_sem=g_recv.at[s, 0],
            device_id=cdev, device_id_type=MESH,
        ).wait_send()

    lane = lax.broadcasted_iota(jnp.int32, (64, 128), 1)
    low = lane < 64

    def interleave(a0, a1):
        f0, f1 = a0.astype(F32), a1.astype(F32)
        first = jnp.where(low, f0, pltpu.roll(f1, 64, 1)).astype(BF)
        second = jnp.where(low, pltpu.roll(f0, 64, 1), f1).astype(BF)
        return first, second

    def zero_fill(i, _):
        zs = jnp.zeros((2, 64, 128), BF)
        zl = jnp.zeros((2, 128, 128), BF)
        fs[1, pl.ds(2 * i, 2)] = zs
        fs[2, pl.ds(2 * i, 2)] = zs
        fl[0, pl.ds(2 * i, 2)] = zl
        fl[1, pl.ds(2 * i, 2)] = zl
        return 0

    lax.fori_loop(0, NQ, zero_fill, 0)

    for i, ref in ((1, lp_ref), (2, up_ref), (3, uu_ref)):
        first, second = interleave(ref[0], ref[1])
        fs[i, 2 * q] = first
        fs[i, 2 * q + 1] = second
    for i, ref in ((0, pl_ref), (1, pu_ref)):
        fl[i, 2 * q] = ref[:, 0:128]
        fl[i, 2 * q + 1] = ref[:, 128:256]
    v[0, p] = jnp.concatenate([pivot_ref[0], pivot_ref[1]], axis=0).T.astype(BF)

    barrier = pltpu.get_barrier_semaphore()
    for d in range(1, NZ):
        signal((panel_of(yl, z_at(d), c), q), barrier)
    signal(ydev, barrier)
    signal(cdev, barrier)
    for d in range(1, 4):
        signal((p, q_at(0, d)), barrier)
        signal((p, q_at(d, 0)), barrier)
    child = p // 16
    for k in range(2):
        src = 16 * k + t
        pl.when(src != p)(lambda src=src: signal((src, q), barrier))
    self_count = jnp.where(jnp.logical_or(p == 0, p == 31), 1, 0)
    pl.semaphore_wait(barrier, 7 + 2 + 6 + 2 - self_count)

    def mcopies(h):
        dst = 2 * (p - 16 * child) + h
        rows = pl.ds(64 * h, 64)
        a = pltpu.make_async_remote_copy(
            src_ref=lu_ref.at[rows], dst_ref=lu_in.at[child],
            send_sem=m_send.at[0, h], recv_sem=m_recv.at[0, child],
            device_id=(dst, q), device_id_type=MESH,
        )
        b = pltpu.make_async_remote_copy(
            src_ref=update_ref.at[rows], dst_ref=upd_in.at[child],
            send_sem=m_send.at[1, h], recv_sem=m_recv.at[1, child],
            device_id=(dst, q), device_id_type=MESH,
        )
        return dst, a, b

    for h in range(2):
        dst, a, b = mcopies(h)

        @pl.when(dst != p)
        def _():
            a.start()
            b.start()

        @pl.when(dst == p)
        def _():
            lu_in[child] = lu_ref[pl.ds(64 * h, 64), :]
            upd_in[child] = update_ref[pl.ds(64 * h, 64), :]

    g_start(0)

    for k in range(2):
        @pl.when(16 * k + t != p)
        def _():
            for i, ref in ((0, lu_in), (1, upd_in)):
                pltpu.make_async_remote_copy(
                    src_ref=ref.at[k], dst_ref=ref.at[k],
                    send_sem=m_send.at[i, 0], recv_sem=m_recv.at[i, k],
                    device_id=cdev, device_id_type=MESH,
                ).wait_recv()

    first, second = interleave(lu_in[0], lu_in[1])
    fs[0, 2 * q] = first
    fs[0, 2 * q + 1] = second
    y_phase(LU)
    g_mid(0)
    x_phase(LU)
    y_phase(PLO)
    y_phase(LP)
    g_end(0)

    half_mask = (lax.rem(lax.broadcasted_iota(jnp.int32, (64, 512), 1), 128) < 64).astype(F32)
    mask_low = half_mask.astype(BF)
    mask_high = (1.0 - half_mask).astype(BF)

    def wide(ref, lead, i):
        return jnp.concatenate([ref[lead, 4 * i + j] for j in range(4)], axis=1)

    def apply_large(s, a):
        def step(i, acc):
            return acc + dot(wide(v, s, i), wide(fl, a, i), NT)
        return lax.fori_loop(0, NP // 4, step, jnp.zeros((128, 128), F32))

    def apply_small(s, a, init):
        def step(i, acc):
            f = wide(fs, a, i)
            both = jnp.concatenate([f * mask_low, f * mask_high], axis=0)
            return acc + dot(wide(v, s, i), both, NT)
        return lax.fori_loop(0, NP // 4, step, init)

    zero = jnp.zeros((128, 128), F32)

    m0 = maps_ref[pl.ds(t, 1), :]
    m1 = maps_ref[pl.ds(16 + t, 1), :]
    lane1 = lax.broadcasted_iota(jnp.int32, (8, 128), 1)
    m0 = jnp.broadcast_to(m0, (8, 128))
    m1 = jnp.broadcast_to(m1, (8, 128))
    even = c == 0
    lo = jnp.where(even, m0, pltpu.roll(m0, 64, 1))
    hi = jnp.where(even, pltpu.roll(m1, 64, 1), m1)
    m = jnp.where(lane1 < 64, lo, hi)[0:1] - 128 * p
    row = lax.broadcasted_iota(jnp.int32, (128, 128), 0)
    select = jnp.where(row == m, 1.0, 0.0).astype(BF)

    upd_t = jnp.concatenate([upd_in[0], upd_in[1]], axis=0).T
    parent_t = parent_ref[...].T

    f_wait(LU)
    u_t = apply_small(0, 0, upd_t)
    s_t = parent_t + dot(u_t.astype(BF), select, NT)
    v[1, p] = s_t.astype(BF)
    g_start(1)

    x_phase(PLO)
    x_phase(LP)
    y_phase(PUP)
    g_mid(1)
    f_wait(LP)
    v[4, p] = apply_small(0, 1, zero).astype(BF)
    g_end(1)
    f_wait(PLO)
    v[2, p] = apply_large(1, 0).astype(BF)
    g_start(2)
    g_start(4)
    x_phase(PUP)
    y_phase(UP)
    y_phase(UU)
    g_mid(2)
    g_end(2)
    g_mid(4)
    f_wait(PUP)
    sol_t = apply_large(2, 1)
    r_t = dot(sol_t.astype(BF), select, NN)
    v[3, p] = r_t.astype(BF)
    g_start(3)
    sol_ref[...] = sol_t.T
    x_phase(UP)
    x_phase(UU)
    g_end(4)
    f_wait(UP)
    acc = apply_small(4, 2, zero)
    g_mid(3)
    g_end(3)
    f_wait(UU)
    acc = apply_small(3, 3, acc)
    out = acc.T
    child_ref[0] = out[0:64]
    child_ref[1] = out[64:128]

    for s in range(5):
        g_drain(s)
    for a in range(6):
        f_drain(a)
    for h in range(2):
        dst, a, b = mcopies(h)

        @pl.when(dst != p)
        def _():
            a.wait_send()
            b.wait_send()


def shards(pivot_rhs, update_rhs, parent_rhs, lower_pivot, lower_update, parent_lower, parent_upper, upper_pivot, upper_update, maps):
    vm = pl.BlockSpec(memory_space=pltpu.VMEM)
    dma = pltpu.SemaphoreType.DMA
    return pl.pallas_call(
        body,
        out_shape=(
            jax.ShapeDtypeStruct((128, 128), F32),
            jax.ShapeDtypeStruct((2, 64, 128), F32),
        ),
        in_specs=[vm] * 10,
        out_specs=(vm, vm),
        scratch_shapes=[
            pltpu.VMEM((5, NP, 128, 128), BF),
            pltpu.VMEM((4, NP, 64, 128), BF),
            pltpu.VMEM((2, NP, 128, 128), BF),
            pltpu.VMEM((2, 64, 128), BF),
            pltpu.VMEM((2, 64, 128), F32),
            pltpu.VMEM((8, 128), F32),
            dma((5,)),
            dma((5, NP)),
            dma((6, 15)),
            dma((6, NQ)),
            dma((2, 2)),
            dma((2, 2)),
        ],
        compiler_params=pltpu.CompilerParams(collective_id=0, has_side_effects=True, vmem_limit_bytes=32 << 20),
    )(
        pivot_rhs, update_rhs, parent_rhs, lower_pivot, lower_update, parent_lower, parent_upper,
        upper_pivot, upper_update, maps.reshape(32, 128),
    )


def solution(mesh):
    placed = (
        P(None, "panel", "rhs"),
        P("panel", "rhs"),
        P("panel", "rhs"),
        P(None, "panel", "rhs"),
        P("panel", "rhs"),
        P("panel", "rhs"),
        P("panel", "rhs"),
        P(None, "panel", "rhs"),
        P(None, "panel", "rhs"),
        P(),
    )
    return jax.shard_map(
        shards,
        mesh=mesh,
        in_specs=placed,
        out_specs=(P("panel", "rhs"), P(None, "panel", "rhs")),
        check_vma=False,
    )
```

time: 353 us -> 106 us (0.30)
  waiting for transfers between devices: 238 us -> 0 us
  Pallas kernels: 0 us -> 95.7 us
  starting transfers between devices: 66.1 us -> 0 us
  local copies, waits for them, and re-layouts: 24.2 us -> 9.2 us
  between operations: 14.3 us -> 0.66 us
  matrix products: 7.12 us -> 0 us
    all_to_all x8 -> x0, waiting for transfers between devices: 179 us -> none  [copy_for_each(): lax.all_to_all(jnp.broadcast_to(shard[None], (peers, *shard.shape)), axis...]
    pallas_call x0 -> x1, Pallas kernels: none -> 95.7 us  [shards(): pl.pallas_call(body, out_shape=(jax.ShapeDtypeStruct((128, 128), F32), ja...]
    all_to_all x8 -> x0, starting transfers between devices: 66 us -> none  [copy_for_each(): lax.all_to_all(jnp.broadcast_to(shard[None], (peers, *shard.shape)), axis...]
    all_gather x2 -> x0, waiting for transfers between devices: 59 us -> none  [sent_together(): lax.all_gather(both, axis, axis=dim, tiled=True)]
    gather x1 -> x0, local copies, waits for them, and re-layouts: 12.1 us -> none  [shards(): remote_rows = jnp.take(solution_all, maps, axis=0).reshape(2, FU, rhs_width)]
    broadcast_in_dim x9 -> x0, local copies, waits for them, and re-layouts: 9.73 us -> none  [the longest x8 9.72 us: copy_for_each(): jnp.broadcast_to(shard[None], (peers, *shard.shape))]
    unnamed x25 -> x22, local copies, waits for them, and re-layouts: 0.99 us -> 9.2 us
    dot_general x7 -> x0, matrix products: 7.12 us -> none  [the longest x4 4.04 us: product(): return jnp.dot(left, right, preferred_element_type=jnp.float32)]
  transfers between devices with their start and end apart: 10 -> 0, of which waited for: 10 -> 0; matrix products, arithmetic and copies ran while one was open for 2% -> 0% of each run, Pallas kernels for 0% -> 0%
where the time goes in v1:
time: 106 us
  Pallas kernels  95.7 us (90%)
  local copies, waits for them, and re-layouts  9.2 us (9%)
    pallas_call x1, Pallas kernels, shards(): pl.pallas_call(body, out_shape=(jax.ShapeDtypeStruct((128, 128), F32), ja...  95.7 us
    unnamed x22, local copies, waits for them, and re-layouts  9.2 us

profile of v1, /device:TPU:1, one launch (start us, length us, event | category | flops | bytes accessed | tf_op | source)
XLA Modules:
  0.0 105.6 jit_solution(5940364297697587542)
XLA Ops:
  0.6 0.0 copy-start
  0.6 0.8 copy-done
  1.5 0.0 copy-start.1
  1.5 0.8 copy-done.1
  2.3 0.0 copy-start.2
  2.3 0.8 copy-done.2
  3.2 0.0 copy-start.3
  3.2 0.8 copy-done.3
  4.0 0.0 copy-start.4
  4.0 0.8 copy-done.4
  4.8 0.0 copy-start.5
  4.8 0.8 copy-done.5
  5.6 0.0 copy-start.6
  5.6 0.8 copy-done.6
  6.4 0.0 copy-start.7
  6.4 0.8 copy-done.7
  7.1 0.0 copy-start.8
  7.1 0.8 copy-done.8
  7.9 0.0 copy-start.9
  7.9 0.7 copy-done.9
  8.6 95.7 %shard_map.113 = (f32[128,128]{1,0:T(8,128)S(1)}, f32[2,64,128]{2,1,0:T(8,128)S(1)}) custom-call(f32[2,64,128]{2,1,0:T(8,128)S(1)} %copy-done, f32[128,128]{1,0:T(8,128)S(1)} %copy-done.1, f32[128,128]{1,0:T(8,128)S(1)} %copy-done.2, bf16[2,64,128]{2,1,0:T(8,128)(2,1)S(1)} %copy-done.5, bf16[128,128]{1,0:T(8,128)(2,1)S(1)} %copy-done.6, ...), custom_call_target="tpu_custom_call" | custom-call | tf_op jit(solution)/shard_map/pallas_call | solution.py:344
  104.3 0.6 copy.14
  105.0 0.6 copy.15
Async XLA Ops:
  0.6 0.8 copy-start
  1.5 0.8 copy-start.1
  2.3 0.8 copy-start.2
  3.2 0.8 copy-start.3
  4.0 0.8 copy-start.4
  4.8 0.8 copy-start.5
  5.6 0.8 copy-start.6
  6.4 0.8 copy-start.7
  7.1 0.8 copy-start.8
  7.9 0.7 copy-start.9

commit v2 on v0

v2 whole, which is shorter than its diff:
```python
import jax
import jax.numpy as jnp
from jax import lax
from jax.experimental import pallas as pl
from jax.experimental.pallas import tpu as pltpu
from jax.sharding import PartitionSpec as P

MESH = pl.DeviceIdType.MESH
BF = jnp.bfloat16
F32 = jnp.float32
NZ = 8
NT = 16
H = 2
W = 64 // H
CONTRACT_LAST = (((1,), (1,)), ((), ()))
CONTRACT_INNER = (((1,), (0,)), ((), ()))
ZORDER = (1, 7, 2, 6, 3, 5, 4)
TURN = (1, 3, 2)

LU, LP, PLO, PUP, UP, UU = range(6)
X, S, M, R, PM = range(5)


def dot(a, b, dims=CONTRACT_LAST):
    return lax.dot_general(a, b, dims, preferred_element_type=F32)


def body(
    pivot_hbm, update_hbm, parent_hbm, lp_hbm, lu_hbm, pl_hbm, pu_hbm, up_hbm, uu_hbm, maps_hbm,
    sol_ref, child_ref,
    v, f_lu, f_lp, f_pl, f_pu, f_up, f_uu,
    lu_ref, update_ref, pivot_ref, parent_ref, maps_ref,
    upd_in, x_out, x_in, u_out, u_in, par_out, par_in, sol_out, sol_in, ch_out, ch_in, acc_ref,
    g_send, g_recv, y_recv, f_send, f_recv, d_send, d_recv, m_send, m_recv, e_send, e_recv, l_sem,
):
    p = lax.axis_index("panel")
    q = lax.axis_index("rhs")
    c = lax.rem(p, 2)
    t = p // 2
    yl = t // NZ
    z = lax.rem(t, NZ)
    x = q // 4
    yh = lax.rem(q, 4)
    factors = (f_lu, f_lp, f_pl, f_pu, f_up, f_uu)

    def z_at(d):
        return lax.rem(z + d, NZ)

    def q_at(dx, dy):
        return lax.rem(x + dx, 4) * 4 + lax.rem(yh + dy, 4)

    def z_dev(d):
        return ((yl * NZ + z_at(d)) * 2 + c, q)

    y_dev = (((1 - yl) * NZ + z) * 2 + c, q)
    c_dev = (2 * t + 1 - c, q)
    move_src = 16 * c + t
    move_dst = 2 * lax.rem(p, 16) + p // 16
    moves = move_src != p

    pairs = [(lu_hbm, lu_ref), (pivot_hbm, pivot_ref), (update_hbm, update_ref), (parent_hbm, parent_ref), (maps_hbm, maps_ref)]
    pairs += [(h, f.at[q, c]) for h, f in ((lp_hbm, f_lp), (pl_hbm, f_pl), (pu_hbm, f_pu), (up_hbm, f_up), (uu_hbm, f_uu))]
    loads = [pltpu.make_async_copy(a, b, l_sem.at[i]) for i, (a, b) in enumerate(pairs)]
    for load in loads:
        load.start()

    barrier = pltpu.get_barrier_semaphore()

    def signal(dev):
        pl.semaphore_signal(barrier, inc=1, device_id=dev, device_id_type=MESH)

    for d in range(1, NZ):
        signal(z_dev(d))
    signal(y_dev)
    signal(c_dev)
    for d in range(1, 4):
        signal((p, q_at(0, d)))
        signal((p, q_at(d, 0)))
    pl.when(moves)(lambda: signal((move_src, q)))

    def needed(a, qq):
        if a in (LP, PLO):
            return qq <= t
        if a in (PUP, UP):
            return qq >= t
        return None

    def when(cond, fn):
        if cond is None:
            fn()
        else:
            pl.when(cond)(fn)

    def f_copy(a, qq, dev):
        block = factors[a].at[qq, c]
        return pltpu.make_async_remote_copy(
            src_ref=block, dst_ref=block, send_sem=f_send.at[a], recv_sem=f_recv.at[a, qq],
            device_id=dev, device_id_type=MESH,
        )

    def d_copy(a, part):
        block = factors[a].at[part, c]
        return pltpu.make_async_remote_copy(
            src_ref=block, dst_ref=block, send_sem=d_send.at[a], recv_sem=d_recv.at[a],
            device_id=c_dev, device_id_type=MESH,
        )

    def send_x(a, qq):
        for dx in TURN:
            f_copy(a, qq, (p, q_at(dx, 0))).start()

    def f_y(a):
        return [
            lambda dy=dy: when(needed(a, q), f_copy(a, q, (p, q_at(0, dy))).start)
            for dy in TURN
        ]

    def f_x(a):
        def go():
            when(needed(a, q), lambda: send_x(a, q))
            d_copy(a, q).start()
        return [go]

    def f_turn(a):
        def step(qq):
            def go():
                f_copy(a, qq, c_dev).wait_recv()
                send_x(a, qq)
            when(needed(a, qq), go)
            d_copy(a, qq).start()
        return [lambda qq=q_at(0, dy): step(qq) for dy in TURN]

    def f_last(a):
        def step(qq):
            when(needed(a, qq), f_copy(a, qq, c_dev).wait_recv)
            d_copy(a, qq).start()
        return [lambda qq=q_at(dx, dy): step(qq) for dy in (0,) + TURN for dx in TURN]

    def f_ready(a):
        d_copy(a, pl.ds(0, NT)).wait_recv()

    def f_drain(a):
        def sent(n):
            part = factors[a].at[pl.ds(0, 3 * n), 0]
            pltpu.make_async_remote_copy(
                src_ref=part, dst_ref=part, send_sem=f_send.at[a], recv_sem=f_recv.at[a, 0],
                device_id=c_dev, device_id_type=MESH,
            ).wait_send()
        if needed(a, q) is None:
            sent(5)
        else:
            column = t - 4 * x + 1 if a in (LP, PLO) else 4 * x + 4 - t
            count = jnp.clip(column, 0, 4) + jnp.where(needed(a, q), 1, 0)
            for n in range(1, 6):
                pl.when(count == n)(lambda n=n: sent(n))
        d_copy(a, pl.ds(0, NT)).wait_send()

    def run(*steps):
        for group in steps:
            for step in group:
                step()

    def g_copy(s, h, tt, dev, sem):
        block = v.at[s, h, tt]
        return pltpu.make_async_remote_copy(
            src_ref=block, dst_ref=block, send_sem=g_send.at[s, h], recv_sem=sem,
            device_id=dev, device_id_type=MESH,
        )

    def g_start(s, h):
        for d in ZORDER:
            g_copy(s, h, t, z_dev(d), g_recv.at[s, h, z]).start()
        g_copy(s, h, t, y_dev, y_recv.at[s, h]).start()

    def g_turn(s, h, *steps):
        steps = [step for group in steps for step in group]
        for i, d in enumerate(ZORDER):
            tt = yl * NZ + z_at(d)
            g_copy(s, h, tt, y_dev, g_recv.at[s, h, z_at(d)]).wait_recv()
            g_copy(s, h, tt, y_dev, y_recv.at[s, h]).start()
            todo = steps[len(steps) * i // 7 : len(steps) * (i + 1) // 7]
            run(todo)

    def g_last(s, h):
        g_copy(s, h, pl.ds((1 - yl) * NZ, NZ), y_dev, y_recv.at[s, h]).wait_recv()

    def g_drain(s, h):
        g_copy(s, h, pl.ds(0, 15), y_dev, y_recv.at[s, h]).wait_send()

    def e_copy(i, src, dst):
        return pltpu.make_async_remote_copy(
            src_ref=src, dst_ref=dst, send_sem=e_send.at[i], recv_sem=e_recv.at[i],
            device_id=c_dev, device_id_type=MESH,
        )

    mine = pl.ds(pl.multiple_of(64 * c, 64), 64)
    other = pl.ds(pl.multiple_of(64 - 64 * c, 64), 64)
    x_ex = e_copy(0, x_out.at[other], x_in)
    u_ex = e_copy(1, u_out.at[other], u_in)
    par_ex = e_copy(2, par_out.at[other], par_in)
    sol_ex = e_copy(3, sol_out, sol_in)
    ch_ex = e_copy(4, ch_out, ch_in)

    first_core = c == 0

    def ordered(own, got):
        return jnp.where(first_core, own, got), jnp.where(first_core, got, own)

    low = lax.broadcasted_iota(jnp.int32, (64, 128), 1) < 64

    def swap_halves(a, b):
        return jnp.where(low, a, pltpu.roll(b, 64, 1)), jnp.where(low, pltpu.roll(a, 64, 1), b)

    with jax.named_scope("prep"):
        loads[1].wait()
        x_out[...] = jnp.concatenate([pivot_ref[0], pivot_ref[1]], axis=0).T.astype(BF).astype(F32)

        def clear(f, i):
            @pl.when(i != q)
            def _():
                f[i, c] = jnp.zeros(f.shape[2:], BF)

        def zero_fill(i, _):
            @pl.when(i > t)
            def _():
                clear(f_lp, i)
                clear(f_pl, i)

            @pl.when(i < t)
            def _():
                clear(f_up, i)
                clear(f_pu, i)

            return 0

        lax.fori_loop(0, NT, zero_fill, 0)
        loads[0].wait()
    with jax.named_scope("barrier"):
        pl.semaphore_wait(barrier, 7 + 2 + 6 + jnp.where(moves, 1, 0))

    own_lu = f_lu.at[q, c]
    lu_move = pltpu.make_async_remote_copy(
        src_ref=lu_ref, dst_ref=f_lu.at[q, p // 16], send_sem=m_send.at[0], recv_sem=m_recv.at[0],
        device_id=(move_dst, q), device_id_type=MESH,
    )
    upd_move = pltpu.make_async_remote_copy(
        src_ref=update_ref, dst_ref=upd_in, send_sem=m_send.at[1], recv_sem=m_recv.at[1],
        device_id=(move_dst, q), device_id_type=MESH,
    )
    lu_arrival = pltpu.make_async_remote_copy(
        src_ref=own_lu, dst_ref=own_lu, send_sem=m_send.at[0], recv_sem=m_recv.at[0],
        device_id=c_dev, device_id_type=MESH,
    )
    x_ex.start()
    pl.when(moves)(lu_move.start)

    @pl.when(jnp.logical_not(moves))
    def _():
        f_lu[q, c] = lu_ref[...]

    with jax.named_scope("x_ex"):
        x_ex.wait_recv()
    x0, x1 = swap_halves(*ordered(x_out[mine, :], x_in[...]))
    xt = jnp.concatenate([x0, x1], axis=1).astype(BF)
    for h in range(H):
        v[X, h, t] = xt[W * h : W * (h + 1)]
        g_start(X, h)

    for load in loads[2:]:
        load.wait()
    run(f_x(PLO), f_x(LP), f_x(PUP))
    pl.when(moves)(upd_move.start)

    @pl.when(jnp.logical_not(moves))
    def _():
        upd_in[...] = update_ref[...]

    par_out[...] = parent_ref[...].T
    par_ex.start()
    with jax.named_scope("w_lu_move"):
        pl.when(moves)(lu_arrival.wait_recv)
    run(f_y(LU), f_x(LU))
    with jax.named_scope("x_turn0"):
        g_turn(X, 0, f_y(PLO), f_turn(LU))
    with jax.named_scope("x_turn1"):
        for h in range(1, H):
            g_turn(X, h)
    with jax.named_scope("w_upd"):
        pl.when(moves)(upd_move.wait_recv)
        u_out[...] = upd_in[...].T
    u_ex.start()

    row = lax.broadcasted_iota(jnp.int32, (256, 128), 0)

    def selection(k):
        return jnp.where(row == maps_ref[pl.ds(16 * k + t, 1), :] - 256 * t, 1.0, 0.0).astype(BF)

    select = (selection(0), selection(1))

    def line(s, h, side):
        first = side * NZ
        return [v[s, h, first + j] for j in range(NZ)], [first + j for j in range(NZ)]

    def apply_parent(s, h, f, side):
        blocks, at = line(s, h, side)
        left = jnp.concatenate(blocks, axis=1)
        right = jnp.concatenate([f[i].reshape(256, 256) for i in at], axis=1)
        return dot(left, right)

    def apply_child(s, h, f, side):
        blocks, at = line(s, h, side)
        out = []
        for k in range(2):
            left = jnp.concatenate([b[:, 128 * k : 128 * (k + 1)] for b in blocks], axis=1)
            if f is f_lu:
                right = jnp.concatenate([f[i, k] for i in at], axis=1)
            else:
                right = jnp.concatenate(
                    [jnp.concatenate([f[i, 0, k], f[i, 1, k]], axis=0) for i in at], axis=1
                )
            out.append(dot(left, right))
        return jnp.concatenate(out, axis=1)

    def both(fn, s, h, f):
        return fn(s, h, f, yl) + fn(s, h, f, 1 - yl)

    run(f_y(LP))
    with jax.named_scope("lu_last"):
        run(f_last(LU)[:6], f_y(PUP), f_last(LU)[6:])
    with jax.named_scope("pl_turn"):
        run(f_turn(PLO))
    with jax.named_scope("x_last"):
        g_last(X, 0)
    with jax.named_scope("lu_ready"):
        f_ready(LU)
    with jax.named_scope("ex_upd_par"):
        par_ex.wait_recv()
        u_ex.wait_recv()
    upd = ordered(u_out[mine, :], u_in[...])
    par = jnp.concatenate(ordered(par_out[mine, :], par_in[...]), axis=1)
    for h in range(H):
        rows = slice(W * h, W * (h + 1))
        if h:
            with jax.named_scope("x_last1"):
                g_last(X, h)
        with jax.named_scope("mm_s"):
            u = both(apply_child, X, h, f_lu)
            u0 = (upd[0][rows] + u[:, :128]).astype(BF)
            u1 = (upd[1][rows] + u[:, 128:]).astype(BF)
            st = par[rows] + (dot(u0, select[0]) + dot(u1, select[1]))
            v[S, h, t] = st.astype(BF)
        g_start(S, h)

    def stage(src, f, a, steps, finish):
        steps = steps if H == 2 else [steps[0] + steps[1]]
        for h in range(H):
            with jax.named_scope("turn%d_%d" % (h, src)):
                g_turn(src, h, steps[h])
        with jax.named_scope("f_last_%d" % src):
            run(f_last(a))
        with jax.named_scope("f_ready_%d" % src):
            f_ready(a)
        for h in range(H):
            with jax.named_scope("mm0_%d" % src):
                acc_ref[...] = apply_parent(src, h, f, yl)
            with jax.named_scope("last%d_%d" % (h, src)):
                g_last(src, h)
            with jax.named_scope("mm1_%d" % src):
                finish(h, acc_ref[...] + apply_parent(src, h, f, 1 - yl))

    def finish_m(h, acc):
        v[M, h, t] = acc.astype(BF)
        g_start(M, h)

    stage(S, f_pl, PLO, [f_turn(LP) + f_x(UP) + f_x(UU), f_y(UP) + f_turn(PUP)], finish_m)

    with jax.named_scope("lp_last"):
        run(f_last(LP))
        f_ready(LP)
    for h in range(H):
        with jax.named_scope("mm_p"):
            v[PM, h, t] = both(apply_child, X, h, f_lp).astype(BF)
        g_start(PM, h)
    sols = []

    def finish_r(h, acc):
        half = acc.astype(BF)
        r = [dot(half, select[k], CONTRACT_INNER) for k in range(2)]
        v[R, h, t] = jnp.concatenate(r, axis=1).astype(BF)
        g_start(R, h)
        sols.append(acc)

    stage(M, f_pu, PUP, [f_y(UU), f_turn(UP)], finish_r)

    sol = jnp.concatenate(sols, axis=0)
    own_sol, their_sol = ordered(sol[:, :128], sol[:, 128:])
    sol_out[...] = their_sol
    sol_ex.start()
    with jax.named_scope("u_turn"):
        run(f_turn(UU))
    with jax.named_scope("p_turn"):
        for h in range(H):
            g_turn(PM, h)
    for h in range(H):
        with jax.named_scope("turn%d_R" % h):
            g_turn(R, h, f_last(UP)[12 // H * h : 12 // H * (h + 1)])
    with jax.named_scope("uu_last"):
        run(f_last(UU))
    with jax.named_scope("p_last"):
        for h in range(H):
            g_last(PM, h)
    with jax.named_scope("up_ready"):
        f_ready(UP)
        f_ready(UU)
    outs = []
    for h in range(H):
        with jax.named_scope("mm_c0"):
            acc_ref[...] = both(apply_child, PM, h, f_up) + apply_child(R, h, f_uu, yl)
        with jax.named_scope("r_last%d" % h):
            g_last(R, h)
        with jax.named_scope("mm_c1"):
            outs.append(acc_ref[...] + apply_child(R, h, f_uu, 1 - yl))
    ch = jnp.concatenate(outs, axis=0)
    own_ch, their_ch = ordered(*swap_halves(ch[:, :128], ch[:, 128:]))
    ch_out[...] = their_ch
    ch_ex.start()
    with jax.named_scope("fin_sol"):
        sol_ex.wait_recv()
        sol_ref[...] = jnp.concatenate(ordered(own_sol, sol_in[...]), axis=0).T
    with jax.named_scope("drain"):
        for s in range(5):
            for h in range(H):
                g_drain(s, h)
        for a in range(6):
            f_drain(a)
        pl.when(moves)(lu_move.wait_send)
        pl.when(moves)(upd_move.wait_send)
        for e in (x_ex, u_ex, par_ex, sol_ex, ch_ex):
            e.wait_send()
    with jax.named_scope("fin_ch"):
        ch_ex.wait_recv()
        out = jnp.concatenate(ordered(own_ch, ch_in[...]), axis=0).T
        child_ref[0] = out[0:64]
        child_ref[1] = out[64:128]


def shards(pivot_rhs, update_rhs, parent_rhs, lower_pivot, lower_update, parent_lower, parent_upper, upper_pivot, upper_update, maps):
    vm = pl.BlockSpec(memory_space=pltpu.VMEM)
    dma = pltpu.SemaphoreType.DMA
    square = pltpu.VMEM((128, 128), F32)
    half = pltpu.VMEM((64, 128), F32)
    child_factor = pltpu.VMEM((NT, 2, 2, 64, 128), BF)
    parent_factor = pltpu.VMEM((NT, 2, 128, 256), BF)
    return pl.pallas_call(
        body,
        out_shape=(
            jax.ShapeDtypeStruct((128, 128), F32),
            jax.ShapeDtypeStruct((2, 64, 128), F32),
        ),
        in_specs=[pl.BlockSpec(memory_space=pltpu.HBM)] * 10,
        out_specs=(vm, vm),
        scratch_shapes=[
            pltpu.VMEM((5, H, NT, W, 256), BF),
            pltpu.VMEM((NT, 2, 128, 128), BF),
            child_factor,
            parent_factor,
            parent_factor,
            child_factor,
            child_factor,
            pltpu.VMEM((128, 128), BF),
            square,
            pltpu.VMEM((2, 64, 128), F32),
            square,
            pltpu.VMEM((32, 128), jnp.int32),
            square, square, half, square, half, square, half, half, half, half, half,
            pltpu.VMEM((W, 256), F32),
            dma((5, H)),
            dma((5, H, NZ)),
            dma((5, H)),
            dma((6,)),
            dma((6, NT)),
            dma((6,)),
            dma((6,)),
            dma((2,)),
            dma((2,)),
            dma((5,)),
            dma((5,)),
            dma((10,)),
        ],
        compiler_params=pltpu.CompilerParams(collective_id=0, has_side_effects=True, vmem_limit_bytes=60 << 20),
    )(
        pivot_rhs, update_rhs, parent_rhs, lower_pivot, lower_update, parent_lower, parent_upper,
        upper_pivot, upper_update, maps.reshape(32, 128),
    )


def solution(mesh):
    placed = (
        P(None, "panel", "rhs"),
        P("panel", "rhs"),
        P("panel", "rhs"),
        P(None, "panel", "rhs"),
        P("panel", "rhs"),
        P("panel", "rhs"),
        P("panel", "rhs"),
        P(None, "panel", "rhs"),
        P(None, "panel", "rhs"),
        P(),
    )
    return jax.shard_map(
        shards,
        mesh=mesh,
        in_specs=placed,
        out_specs=(P("panel", "rhs"), P(None, "panel", "rhs")),
        check_vma=False,
    )
```

time: 353 us -> 79.9 us (0.23)
  waiting for transfers between devices: 238 us -> 0 us
  Pallas kernels: 0 us -> 76.8 us
  starting transfers between devices: 66.1 us -> 0 us
  local copies, waits for them, and re-layouts: 24.2 us -> 2.14 us
  between operations: 14.3 us -> 0.65 us
  matrix products: 7.12 us -> 0 us
    all_to_all x8 -> x0, waiting for transfers between devices: 179 us -> none  [copy_for_each(): lax.all_to_all(jnp.broadcast_to(shard[None], (peers, *shard.shape)), axis...]
    pallas_call x0 -> x1, Pallas kernels: none -> 76.8 us  [shards(): pl.pallas_call(body, out_shape=(jax.ShapeDtypeStruct((128, 128), F32), ja...]
    all_to_all x8 -> x0, starting transfers between devices: 66 us -> none  [copy_for_each(): lax.all_to_all(jnp.broadcast_to(shard[None], (peers, *shard.shape)), axis...]
    all_gather x2 -> x0, waiting for transfers between devices: 59 us -> none  [sent_together(): lax.all_gather(both, axis, axis=dim, tiled=True)]
    gather x1 -> x0, local copies, waits for them, and re-layouts: 12.1 us -> none  [shards(): remote_rows = jnp.take(solution_all, maps, axis=0).reshape(2, FU, rhs_width)]
    broadcast_in_dim x9 -> x0, local copies, waits for them, and re-layouts: 9.73 us -> none  [the longest x8 9.72 us: copy_for_each(): jnp.broadcast_to(shard[None], (peers, *shard.shape))]
    dot_general x7 -> x0, matrix products: 7.12 us -> none  [the longest x4 4.04 us: product(): return jnp.dot(left, right, preferred_element_type=jnp.float32)]
  transfers between devices with their start and end apart: 10 -> 0, of which waited for: 10 -> 0; matrix products, arithmetic and copies ran while one was open for 2% -> 0% of each run, Pallas kernels for 0% -> 0%
where the time goes in v2:
time: 79.9 us; the launch traced here: 79.5 us
  Pallas kernels  76.8 us (96%)
  local copies, waits for them, and re-layouts  2.14 us (3%)
    pallas_call x1, Pallas kernels, shards(): pl.pallas_call(body, out_shape=(jax.ShapeDtypeStruct((128, 128), F32), ja...  76.8 us
    unnamed x4, local copies, waits for them, and re-layouts  2.14 us

profile of v2, /device:TPU:1, one launch (start us, length us, event | category | flops | bytes accessed | tf_op | source)
XLA Modules:
  0.0 79.5 jit_solution(3859736856580605374)
XLA Ops:
  0.6 76.8 %shard_map.113 = (f32[128,128]{1,0:T(8,128)}, f32[2,64,128]{2,1,0:T(8,128)}) custom-call(f32[2,64,128]{2,1,0:T(8,128)} %pivot_hbm.1, f32[128,128]{1,0:T(8,128)} %update_hbm.1, f32[128,128]{1,0:T(8,128)} %parent_hbm.1, bf16[2,64,128]{2,1,0:T(8,128)(2,1)} %lp_hbm.1, bf16[128,128]{1,0:T(8,128)(2,1)} %lu_hbm.1, bf16[128,256]{1,0:T(8,128)(2,1)} %pl_hbm.1, ...), custom_call_target="tpu_custom_call" | custom-call | tf_op jit(solution)/shard_map/pallas_call | solution.py:454
  77.4 0.0 copy-start
  77.4 1.5 %copy.14 = f32[128,128]{1,0:T(8,128)} copy(f32[128,128]{1,0:T(8,128)} %get-tuple-element.4) | data formatting | bytes 131072
  78.9 0.0 copy-done
  78.9 0.6 copy.15
Async XLA Ops:
  77.4 1.5 %copy-start = (f32[2,64,128]{2,1,0:T(8,128)S(1)}, f32[2,64,128]{2,1,0:T(8,128)}, u32[]{:S(2)}) copy-start(f32[2,64,128]{2,1,0:T(8,128)} %get-tuple-element.5) | copy-start | bytes 196612

commit v3 on v2

--- a/solution.py
+++ b/solution.py
@@ -14,11 +14,12 @@
 W = 64 // H
 CONTRACT_LAST = (((1,), (1,)), ((), ()))
 CONTRACT_INNER = (((1,), (0,)), ((), ()))
-ZORDER = (1, 7, 2, 6, 3, 5, 4)
+NEAR = (2, 6, 1, 7)
 TURN = (1, 3, 2)
 
 LU, LP, PLO, PUP, UP, UU = range(6)
 X, S, M, R, PM = range(5)
+SLOT = (0, 1, 0, 1, 2)
 
 
 def dot(a, b, dims=CONTRACT_LAST):
@@ -36,6 +37,7 @@
     p = lax.axis_index("panel")
     q = lax.axis_index("rhs")
     c = lax.rem(p, 2)
+    first_core = c == 0
     t = p // 2
     yl = t // NZ
     z = lax.rem(t, NZ)
@@ -52,6 +54,9 @@
     def z_dev(d):
         return ((yl * NZ + z_at(d)) * 2 + c, q)
 
+    def diagonal(d):
+        return (((1 - yl) * NZ + z_at(d)) * 2 + c, q)
+
     y_dev = (((1 - yl) * NZ + z) * 2 + c, q)
     c_dev = (2 * t + 1 - c, q)
     move_src = 16 * c + t
@@ -69,8 +74,9 @@
     def signal(dev):
         pl.semaphore_signal(barrier, inc=1, device_id=dev, device_id_type=MESH)
 
-    for d in range(1, NZ):
+    for d in NEAR:
         signal(z_dev(d))
+        signal(diagonal(d))
     signal(y_dev)
     signal(c_dev)
     for d in range(1, 4):
@@ -163,29 +169,56 @@
     def g_copy(s, h, tt, dev, sem):
         block = v.at[s, h, tt]
         return pltpu.make_async_remote_copy(
-            src_ref=block, dst_ref=block, send_sem=g_send.at[s, h], recv_sem=sem,
+            src_ref=block, dst_ref=block, send_sem=g_send.at[0], recv_sem=sem,
             device_id=dev, device_id_type=MESH,
         )
 
     def g_start(s, h):
-        for d in ZORDER:
-            g_copy(s, h, t, z_dev(d), g_recv.at[s, h, z]).start()
+        for d in NEAR:
+            g_copy(s, h, t, z_dev(d), g_recv.at[SLOT[s], h, NEAR.index(NZ - d)]).start()
         g_copy(s, h, t, y_dev, y_recv.at[s, h]).start()
 
-    def g_turn(s, h, *steps):
-        steps = [step for group in steps for step in group]
-        for i, d in enumerate(ZORDER):
+    def g_turn(s, h, steps=()):
+        far = g_recv.at[SLOT[s], h, 4]
+        for i, d in enumerate(NEAR):
             tt = yl * NZ + z_at(d)
-            g_copy(s, h, tt, y_dev, g_recv.at[s, h, z_at(d)]).wait_recv()
+            g_copy(s, h, tt, y_dev, g_recv.at[SLOT[s], h, i]).wait_recv()
+
+            def relay(e):
+                g_copy(s, h, tt, z_dev(e), far).start()
+                g_copy(s, h, tt, diagonal(e), y_recv.at[s, h]).start()
+
+            if d == 2:
+                relay(7)
+                pl.when(first_core)(lambda: relay(6))
+            if d == 6:
+                relay(1)
+                pl.when(jnp.logical_not(first_core))(lambda: relay(2))
             g_copy(s, h, tt, y_dev, y_recv.at[s, h]).start()
-            todo = steps[len(steps) * i // 7 : len(steps) * (i + 1) // 7]
-            run(todo)
+            run(steps[len(steps) * i // 4 : len(steps) * (i + 1) // 4])
+
+    def g_far(s, h):
+        g_copy(s, h, pl.ds(0, 3), y_dev, g_recv.at[SLOT[s], h, 4]).wait_recv()
+
+    def turns(s, *steps):
+        for h in range(H):
+            with jax.named_scope("near%d_%d" % (h, s)):
+                g_turn(s, h, steps[h] if h < len(steps) else ())
+
+    def fars(s):
+        for h in range(H):
+            with jax.named_scope("far%d_%d" % (h, s)):
+                g_far(s, h)
 
     def g_last(s, h):
         g_copy(s, h, pl.ds((1 - yl) * NZ, NZ), y_dev, y_recv.at[s, h]).wait_recv()
 
-    def g_drain(s, h):
-        g_copy(s, h, pl.ds(0, 15), y_dev, y_recv.at[s, h]).wait_send()
+    def g_drain():
+        part = v.at[:, :, pl.ds(0, 15)]
+        pltpu.make_async_remote_copy(
+            src_ref=part, dst_ref=part, send_sem=g_send.at[0], recv_sem=y_recv.at[0, 0],
+            device_id=y_dev, device_id_type=MESH,
+        ).wait_send()
 
     def e_copy(i, src, dst):
         return pltpu.make_async_remote_copy(
@@ -201,7 +234,6 @@
     sol_ex = e_copy(3, sol_out, sol_in)
     ch_ex = e_copy(4, ch_out, ch_in)
 
-    first_core = c == 0
 
     def ordered(own, got):
         return jnp.where(first_core, own, got), jnp.where(first_core, got, own)
@@ -215,28 +247,9 @@
         loads[1].wait()
         x_out[...] = jnp.concatenate([pivot_ref[0], pivot_ref[1]], axis=0).T.astype(BF).astype(F32)
 
-        def clear(f, i):
-            @pl.when(i != q)
-            def _():
-                f[i, c] = jnp.zeros(f.shape[2:], BF)
-
-        def zero_fill(i, _):
-            @pl.when(i > t)
-            def _():
-                clear(f_lp, i)
-                clear(f_pl, i)
-
-            @pl.when(i < t)
-            def _():
-                clear(f_up, i)
-                clear(f_pu, i)
-
-            return 0
-
-        lax.fori_loop(0, NT, zero_fill, 0)
         loads[0].wait()
     with jax.named_scope("barrier"):
-        pl.semaphore_wait(barrier, 7 + 2 + 6 + jnp.where(moves, 1, 0))
+        pl.semaphore_wait(barrier, 8 + 2 + 6 + jnp.where(moves, 1, 0))
 
     own_lu = f_lu.at[q, c]
     lu_move = pltpu.make_async_remote_copy(
@@ -269,6 +282,25 @@
     for load in loads[2:]:
         load.wait()
     run(f_x(PLO), f_x(LP), f_x(PUP))
+    def clear(f, i):
+        @pl.when(i != q)
+        def _():
+            f[i, c] = jnp.zeros(f.shape[2:], BF)
+
+    def zero_fill(i, _):
+        @pl.when(i > t)
+        def _():
+            clear(f_lp, i)
+            clear(f_pl, i)
+
+        @pl.when(i < t)
+        def _():
+            clear(f_up, i)
+            clear(f_pu, i)
+
+        return 0
+
+    lax.fori_loop(0, NT, zero_fill, 0)
     pl.when(moves)(upd_move.start)
 
     @pl.when(jnp.logical_not(moves))
@@ -280,11 +312,8 @@
     with jax.named_scope("w_lu_move"):
         pl.when(moves)(lu_arrival.wait_recv)
     run(f_y(LU), f_x(LU))
-    with jax.named_scope("x_turn0"):
-        g_turn(X, 0, f_y(PLO), f_turn(LU))
-    with jax.named_scope("x_turn1"):
-        for h in range(1, H):
-            g_turn(X, h)
+    turns(X, f_y(PLO), f_turn(LU))
+    fars(X)
     with jax.named_scope("w_upd"):
         pl.when(moves)(upd_move.wait_recv)
         u_out[...] = upd_in[...].T
@@ -352,35 +381,31 @@
         g_start(S, h)
 
     def stage(src, f, a, steps, finish):
-        steps = steps if H == 2 else [steps[0] + steps[1]]
-        for h in range(H):
-            with jax.named_scope("turn%d_%d" % (h, src)):
-                g_turn(src, h, steps[h])
+        turns(src, *steps[:2])
         with jax.named_scope("f_last_%d" % src):
             run(f_last(a))
+        run(*steps[2:])
+        fars(src)
         with jax.named_scope("f_ready_%d" % src):
             f_ready(a)
-        for h in range(H):
-            with jax.named_scope("mm0_%d" % src):
-                acc_ref[...] = apply_parent(src, h, f, yl)
+        with jax.named_scope("mm0_%d" % src):
+            for h in range(H):
+                acc_ref[h] = apply_parent(src, h, f, yl)
+        for h in range(H):
+            if h == 0 and src == M:
+                with jax.named_scope("uu_turn"):
+                    run(f_turn(UU))
             with jax.named_scope("last%d_%d" % (h, src)):
                 g_last(src, h)
             with jax.named_scope("mm1_%d" % src):
-                finish(h, acc_ref[...] + apply_parent(src, h, f, 1 - yl))
+                finish(h, acc_ref[h] + apply_parent(src, h, f, 1 - yl))
 
     def finish_m(h, acc):
         v[M, h, t] = acc.astype(BF)
         g_start(M, h)
 
-    stage(S, f_pl, PLO, [f_turn(LP) + f_x(UP) + f_x(UU), f_y(UP) + f_turn(PUP)], finish_m)
-
-    with jax.named_scope("lp_last"):
-        run(f_last(LP))
-        f_ready(LP)
-    for h in range(H):
-        with jax.named_scope("mm_p"):
-            v[PM, h, t] = both(apply_child, X, h, f_lp).astype(BF)
-        g_start(PM, h)
+    stage(S, f_pl, PLO, [f_turn(LP) + f_x(UP) + f_x(UU), f_turn(PUP), f_y(UP)], finish_m)
+
     sols = []
 
     def finish_r(h, acc):
@@ -390,22 +415,33 @@
         g_start(R, h)
         sols.append(acc)
 
-    stage(M, f_pu, PUP, [f_y(UU), f_turn(UP)], finish_r)
+    def pm_start():
+        with jax.named_scope("lp_last"):
+            run(f_last(LP))
+            f_ready(LP)
+        for h in range(H):
+            with jax.named_scope("mm_p"):
+                v[PM, h, t] = both(apply_child, X, h, f_lp).astype(BF)
+            g_start(PM, h)
+
+    def pm_near():
+        with jax.named_scope("pm_near"):
+            for h in range(H):
+                g_turn(PM, h)
+
+    run(f_y(UU))
+    stage(M, f_pu, PUP, [[], f_turn(UP), [pm_start]], finish_r)
+    pm_near()
 
     sol = jnp.concatenate(sols, axis=0)
     own_sol, their_sol = ordered(sol[:, :128], sol[:, 128:])
     sol_out[...] = their_sol
     sol_ex.start()
-    with jax.named_scope("u_turn"):
-        run(f_turn(UU))
-    with jax.named_scope("p_turn"):
-        for h in range(H):
-            g_turn(PM, h)
-    for h in range(H):
-        with jax.named_scope("turn%d_R" % h):
-            g_turn(R, h, f_last(UP)[12 // H * h : 12 // H * (h + 1)])
-    with jax.named_scope("uu_last"):
-        run(f_last(UU))
+    turns(R, f_last(UP), f_last(UU))
+    fars(R)
+    with jax.named_scope("pm_far"):
+        for h in range(H):
+            g_far(PM, h)
     with jax.named_scope("p_last"):
         for h in range(H):
             g_last(PM, h)
@@ -413,13 +449,14 @@
         f_ready(UP)
         f_ready(UU)
     outs = []
+    with jax.named_scope("mm_c0"):
+        for h in range(H):
+            acc_ref[h] = both(apply_child, PM, h, f_up) + apply_child(R, h, f_uu, yl)
     for h in range(H):
-        with jax.named_scope("mm_c0"):
-            acc_ref[...] = both(apply_child, PM, h, f_up) + apply_child(R, h, f_uu, yl)
         with jax.named_scope("r_last%d" % h):
             g_last(R, h)
         with jax.named_scope("mm_c1"):
-            outs.append(acc_ref[...] + apply_child(R, h, f_uu, 1 - yl))
+            outs.append(acc_ref[h] + apply_child(R, h, f_uu, 1 - yl))
     ch = jnp.concatenate(outs, axis=0)
     own_ch, their_ch = ordered(*swap_halves(ch[:, :128], ch[:, 128:]))
     ch_out[...] = their_ch
@@ -428,9 +465,7 @@
         sol_ex.wait_recv()
         sol_ref[...] = jnp.concatenate(ordered(own_sol, sol_in[...]), axis=0).T
     with jax.named_scope("drain"):
-        for s in range(5):
-            for h in range(H):
-                g_drain(s, h)
+        g_drain()
         for a in range(6):
             f_drain(a)
         pl.when(moves)(lu_move.wait_send)
@@ -473,9 +508,9 @@
             square,
             pltpu.VMEM((32, 128), jnp.int32),
             square, square, half, square, half, square, half, half, half, half, half,
-            pltpu.VMEM((W, 256), F32),
-            dma((5, H)),
-            dma((5, H, NZ)),
+            pltpu.VMEM((H, W, 256), F32),
+            dma((1,)),
+            dma((3, H, 5)),
             dma((5, H)),
             dma((6,)),
             dma((6, NT)),

time: 79.9 us -> 76.3 us (0.955)
  Pallas kernels: 76.8 us -> 73.3 us
    pallas_call x1, Pallas kernels: 76.8 us -> 73.3 us  [shards(): pl.pallas_call(body, out_shape=(jax.ShapeDtypeStruct((128, 128), F32), ja...]
where the time goes in v3:
time: 76.3 us; the launch traced here: 76.1 us
  Pallas kernels  73.3 us (96%)
  local copies, waits for them, and re-layouts  2.14 us (3%)
    pallas_call x1, Pallas kernels, shards(): pl.pallas_call(body, out_shape=(jax.ShapeDtypeStruct((128, 128), F32), ja...  73.3 us
    unnamed x4, local copies, waits for them, and re-layouts  2.14 us

profile of v3, /device:TPU:1, one launch (start us, length us, event | category | flops | bytes accessed | tf_op | source)
XLA Modules:
  0.0 76.1 jit_solution(14883015420140245208)
XLA Ops:
  0.6 73.3 %shard_map.113 = (f32[128,128]{1,0:T(8,128)}, f32[2,64,128]{2,1,0:T(8,128)}) custom-call(f32[2,64,128]{2,1,0:T(8,128)} %pivot_hbm.1, f32[128,128]{1,0:T(8,128)} %update_hbm.1, f32[128,128]{1,0:T(8,128)} %parent_hbm.1, bf16[2,64,128]{2,1,0:T(8,128)(2,1)} %lp_hbm.1, bf16[128,128]{1,0:T(8,128)(2,1)} %lu_hbm.1, bf16[128,256]{1,0:T(8,128)(2,1)} %pl_hbm.1, ...), custom_call_target="tpu_custom_call" | custom-call | tf_op jit(solution)/shard_map/pallas_call | solution.py:489
  74.0 0.0 copy-start
  74.0 1.5 %copy.14 = f32[128,128]{1,0:T(8,128)} copy(f32[128,128]{1,0:T(8,128)} %get-tuple-element.4) | data formatting | bytes 131072
  75.5 0.0 copy-done
  75.5 0.6 copy.15
Async XLA Ops:
  74.0 1.5 %copy-start = (f32[2,64,128]{2,1,0:T(8,128)S(1)}, f32[2,64,128]{2,1,0:T(8,128)}, u32[]{:S(2)}) copy-start(f32[2,64,128]{2,1,0:T(8,128)} %get-tuple-element.5) | copy-start | bytes 196612

commit v4 on v3

--- a/solution.py
+++ b/solution.py
@@ -97,12 +97,15 @@
         else:
             pl.when(cond)(fn)
 
-    def f_copy(a, qq, dev):
-        block = factors[a].at[qq, c]
+    def f_copy(a, part, dev, i):
+        block = factors[a].at[part, c]
         return pltpu.make_async_remote_copy(
-            src_ref=block, dst_ref=block, send_sem=f_send.at[a], recv_sem=f_recv.at[a, qq],
+            src_ref=block, dst_ref=block, send_sem=f_send.at[a], recv_sem=f_recv.at[a, i],
             device_id=dev, device_id_type=MESH,
         )
+
+    def in_column(a, xx):
+        return jnp.clip(t - 4 * xx + 1 if a in (LP, PLO) else 4 * xx + 4 - t, 0, 4)
 
     def d_copy(a, part):
         block = factors[a].at[part, c]
@@ -113,11 +116,11 @@
 
     def send_x(a, qq):
         for dx in TURN:
-            f_copy(a, qq, (p, q_at(dx, 0))).start()
+            f_copy(a, qq, (p, q_at(dx, 0)), 3 + TURN.index(4 - dx)).start()
 
     def f_y(a):
         return [
-            lambda dy=dy: when(needed(a, q), f_copy(a, q, (p, q_at(0, dy))).start)
+            lambda dy=dy: when(needed(a, q), f_copy(a, q, (p, q_at(0, dy)), TURN.index(4 - dy)).start)
             for dy in TURN
         ]
 
@@ -128,19 +131,29 @@
         return [go]
 
     def f_turn(a):
-        def step(qq):
+        def step(dy):
+            qq = q_at(0, dy)
+
             def go():
-                f_copy(a, qq, c_dev).wait_recv()
+                f_copy(a, qq, c_dev, TURN.index(dy)).wait_recv()
                 send_x(a, qq)
             when(needed(a, qq), go)
             d_copy(a, qq).start()
-        return [lambda qq=q_at(0, dy): step(qq) for dy in TURN]
+        return [lambda dy=dy: step(dy) for dy in TURN]
 
     def f_last(a):
-        def step(qq):
-            when(needed(a, qq), f_copy(a, qq, c_dev).wait_recv)
-            d_copy(a, qq).start()
-        return [lambda qq=q_at(dx, dy): step(qq) for dy in (0,) + TURN for dx in TURN]
+        def step(dx):
+            xx = lax.rem(x + dx, 4)
+
+            def arrived(n):
+                f_copy(a, pl.ds(4 * xx, n), c_dev, 3 + TURN.index(dx)).wait_recv()
+            if needed(a, q) is None:
+                arrived(4)
+            else:
+                for n in range(1, 5):
+                    pl.when(in_column(a, xx) == n)(lambda n=n: arrived(n))
+            d_copy(a, pl.ds(4 * xx, 4)).start()
+        return [lambda dx=dx: step(dx) for dx in TURN]
 
     def f_ready(a):
         d_copy(a, pl.ds(0, NT)).wait_recv()
@@ -155,8 +168,7 @@
         if needed(a, q) is None:
             sent(5)
         else:
-            column = t - 4 * x + 1 if a in (LP, PLO) else 4 * x + 4 - t
-            count = jnp.clip(column, 0, 4) + jnp.where(needed(a, q), 1, 0)
+            count = in_column(a, x) + jnp.where(needed(a, q), 1, 0)
             for n in range(1, 6):
                 pl.when(count == n)(lambda n=n: sent(n))
         d_copy(a, pl.ds(0, NT)).wait_send()
@@ -355,7 +367,7 @@
 
     run(f_y(LP))
     with jax.named_scope("lu_last"):
-        run(f_last(LU)[:6], f_y(PUP), f_last(LU)[6:])
+        run(f_last(LU)[:2], f_y(PUP), f_last(LU)[2:])
     with jax.named_scope("pl_turn"):
         run(f_turn(PLO))
     with jax.named_scope("x_last"):
@@ -392,9 +404,9 @@
             for h in range(H):
                 acc_ref[h] = apply_parent(src, h, f, yl)
         for h in range(H):
-            if h == 0 and src == M:
-                with jax.named_scope("uu_turn"):
-                    run(f_turn(UU))
+            if h == 0:
+                with jax.named_scope("hook_%d" % src):
+                    run(f_turn(UU) + [pm_near] if src == M else f_last(LP))
             with jax.named_scope("last%d_%d" % (h, src)):
                 g_last(src, h)
             with jax.named_scope("mm1_%d" % src):
@@ -416,12 +428,7 @@
         sols.append(acc)
 
     def pm_start():
-        with jax.named_scope("lp_last"):
-            run(f_last(LP))
-            f_ready(LP)
-        for h in range(H):
-            with jax.named_scope("mm_p"):
-                v[PM, h, t] = both(apply_child, X, h, f_lp).astype(BF)
+        for h in range(H):
             g_start(PM, h)
 
     def pm_near():
@@ -430,8 +437,12 @@
                 g_turn(PM, h)
 
     run(f_y(UU))
+    with jax.named_scope("lp_ready"):
+        f_ready(LP)
+    with jax.named_scope("mm_p"):
+        for h in range(H):
+            v[PM, h, t] = both(apply_child, X, h, f_lp).astype(BF)
     stage(M, f_pu, PUP, [[], f_turn(UP), [pm_start]], finish_r)
-    pm_near()
 
     sol = jnp.concatenate(sols, axis=0)
     own_sol, their_sol = ordered(sol[:, :128], sol[:, 128:])
@@ -513,7 +524,7 @@
             dma((3, H, 5)),
             dma((5, H)),
             dma((6,)),
-            dma((6, NT)),
+            dma((6, 6)),
             dma((6,)),
             dma((6,)),
             dma((2,)),

time: 76.3 us -> 74.7 us (0.979)
  Pallas kernels: 73.3 us -> 71.7 us
    pallas_call x1, Pallas kernels: 73.3 us -> 71.7 us  [shards(): pl.pallas_call(body, out_shape=(jax.ShapeDtypeStruct((128, 128), F32), ja...]
where the time goes in v4:
time: 74.7 us; the launch traced here: 74.5 us
  Pallas kernels  71.7 us (96%)
  local copies, waits for them, and re-layouts  2.14 us (3%)
    pallas_call x1, Pallas kernels, shards(): pl.pallas_call(body, out_shape=(jax.ShapeDtypeStruct((128, 128), F32), ja...  71.7 us
    unnamed x4, local copies, waits for them, and re-layouts  2.14 us

profile of v4, /device:TPU:1, one launch (start us, length us, event | category | flops | bytes accessed | tf_op | source)
XLA Modules:
  0.0 74.5 jit_solution(11377000774060672767)
XLA Ops:
  0.6 71.7 %shard_map.113 = (f32[128,128]{1,0:T(8,128)}, f32[2,64,128]{2,1,0:T(8,128)}) custom-call(f32[2,64,128]{2,1,0:T(8,128)} %pivot_hbm.1, f32[128,128]{1,0:T(8,128)} %update_hbm.1, f32[128,128]{1,0:T(8,128)} %parent_hbm.1, bf16[2,64,128]{2,1,0:T(8,128)(2,1)} %lp_hbm.1, bf16[128,128]{1,0:T(8,128)(2,1)} %lu_hbm.1, bf16[128,256]{1,0:T(8,128)(2,1)} %pl_hbm.1, ...), custom_call_target="tpu_custom_call" | custom-call | tf_op jit(solution)/shard_map/pallas_call | solution.py:500
  72.3 0.0 copy-start
  72.3 1.5 %copy.14 = f32[128,128]{1,0:T(8,128)} copy(f32[128,128]{1,0:T(8,128)} %get-tuple-element.4) | data formatting | bytes 131072
  73.8 0.0 copy-done
  73.8 0.6 copy.15
Async XLA Ops:
  72.3 1.5 %copy-start = (f32[2,64,128]{2,1,0:T(8,128)S(1)}, f32[2,64,128]{2,1,0:T(8,128)}, u32[]{:S(2)}) copy-start(f32[2,64,128]{2,1,0:T(8,128)} %get-tuple-element.5) | copy-start | bytes 196612

commit v5 on v4

--- a/solution.py
+++ b/solution.py
@@ -325,6 +325,7 @@
         pl.when(moves)(lu_arrival.wait_recv)
     run(f_y(LU), f_x(LU))
     turns(X, f_y(PLO), f_turn(LU))
+    run(f_y(LP), f_y(PUP))
     fars(X)
     with jax.named_scope("w_upd"):
         pl.when(moves)(upd_move.wait_recv)
@@ -365,9 +366,8 @@
     def both(fn, s, h, f):
         return fn(s, h, f, yl) + fn(s, h, f, 1 - yl)
 
-    run(f_y(LP))
     with jax.named_scope("lu_last"):
-        run(f_last(LU)[:2], f_y(PUP), f_last(LU)[2:])
+        run(f_last(LU))
     with jax.named_scope("pl_turn"):
         run(f_turn(PLO))
     with jax.named_scope("x_last"):
@@ -406,7 +406,7 @@
         for h in range(H):
             if h == 0:
                 with jax.named_scope("hook_%d" % src):
-                    run(f_turn(UU) + [pm_near] if src == M else f_last(LP))
+                    run([pm_near] if src == M else f_last(LP))
             with jax.named_scope("last%d_%d" % (h, src)):
                 g_last(src, h)
             with jax.named_scope("mm1_%d" % src):
@@ -416,7 +416,8 @@
         v[M, h, t] = acc.astype(BF)
         g_start(M, h)
 
-    stage(S, f_pl, PLO, [f_turn(LP) + f_x(UP) + f_x(UU), f_turn(PUP), f_y(UP)], finish_m)
+    run(f_y(UP))
+    stage(S, f_pl, PLO, [f_turn(LP) + f_x(UP) + f_x(UU), f_turn(PUP), f_y(UU)], finish_m)
 
     sols = []
 
@@ -436,13 +437,12 @@
             for h in range(H):
                 g_turn(PM, h)
 
-    run(f_y(UU))
     with jax.named_scope("lp_ready"):
         f_ready(LP)
     with jax.named_scope("mm_p"):
         for h in range(H):
             v[PM, h, t] = both(apply_child, X, h, f_lp).astype(BF)
-    stage(M, f_pu, PUP, [[], f_turn(UP), [pm_start]], finish_r)
+    stage(M, f_pu, PUP, [f_turn(UP), f_turn(UU), [pm_start]], finish_r)
 
     sol = jnp.concatenate(sols, axis=0)
     own_sol, their_sol = ordered(sol[:, :128], sol[:, 128:])

time: 74.7 us -> 74.7 us (level)
  no operation moved by 1% of the time
where the time goes in v5:
time: 74.7 us; the launch traced here: 74.4 us
  Pallas kernels  71.7 us (96%)
  local copies, waits for them, and re-layouts  2.14 us (3%)
    pallas_call x1, Pallas kernels, shards(): pl.pallas_call(body, out_shape=(jax.ShapeDtypeStruct((128, 128), F32), ja...  71.7 us
    unnamed x4, local copies, waits for them, and re-layouts  2.14 us

profile of v5, /device:TPU:1, one launch (start us, length us, event | category | flops | bytes accessed | tf_op | source)
XLA Modules:
  0.0 74.4 jit_solution(15204180766234908729)
XLA Ops:
  0.6 71.7 %shard_map.113 = (f32[128,128]{1,0:T(8,128)}, f32[2,64,128]{2,1,0:T(8,128)}) custom-call(f32[2,64,128]{2,1,0:T(8,128)} %pivot_hbm.1, f32[128,128]{1,0:T(8,128)} %update_hbm.1, f32[128,128]{1,0:T(8,128)} %parent_hbm.1, bf16[2,64,128]{2,1,0:T(8,128)(2,1)} %lp_hbm.1, bf16[128,128]{1,0:T(8,128)(2,1)} %lu_hbm.1, bf16[128,256]{1,0:T(8,128)(2,1)} %pl_hbm.1, ...), custom_call_target="tpu_custom_call" | custom-call | tf_op jit(solution)/shard_map/pallas_call | solution.py:500
  72.3 0.0 copy-start
  72.3 1.5 %copy.14 = f32[128,128]{1,0:T(8,128)} copy(f32[128,128]{1,0:T(8,128)} %get-tuple-element.4) | data formatting | bytes 131072
  73.8 0.0 copy-done
  73.8 0.6 copy.15
Async XLA Ops:
  72.3 1.5 %copy-start = (f32[2,64,128]{2,1,0:T(8,128)S(1)}, f32[2,64,128]{2,1,0:T(8,128)}, u32[]{:S(2)}) copy-start(f32[2,64,128]{2,1,0:T(8,128)} %get-tuple-element.5) | copy-start | bytes 196612
